TPU v7x, 32 devices: a whole 2x2x4 slice. The times are simulated.
32 devices in a mesh: groups: 2 (over y), gz: 8 (over z, x), ea: 2 (over core).
Axes of the slice: x: 2, y: 2, z: 4, core: 2. Of those that a mesh axis runs over, the one named last changes fastest.
Arguments:
- eigvec: bfloat16 [96, 3, 2, 16, 512], P('ea', None, None, ('groups', 'gz')), parts along dimension 3, may hold values from -3 to 3
- links: float32 [3, 3, 3, 2, 16, 512], P(None, None, None, None, ('groups', 'gz')), parts along dimension 4, may hold values from -1.8 to 1.8
- momentum: int32 [6], P('groups'), parts along dimension 0, may hold values from -2 to 2
- weights: int32 [6], P('groups'), parts along dimension 0, may hold values from 1 to 3
- spins: int32 [6, 2], P('groups'), parts along dimension 0, may hold values from 0 to 3
- peram: float32 [8, 4, 2, 96, 96], P('groups'), parts along dimension 0, may hold values from -0.4375 to 0.4375
Outputs:
- baryon_block: float32 [4, 96, 9216], P('groups', 'ea', 'gz'), parts along dimension 0
There are 2 independent parts, one for each index of `groups`. A program takes and returns all parts, laid end to end along the dimension named above; each array names one. Nothing has to cross between parts.
All inputs are finite; a program needn't handle non-finite values.
Results may differ from a plain program's by a relative error of at most 0.0045.
Values may be sent and summed in bfloat16 or wider, within the bound.
A program may use at most 64 MiB of HBM per device.

v0:
```python
import functools
import math

import jax
import jax.numpy as jnp
from jax import lax
from jax.experimental import pallas as pl
from jax.experimental.pallas import tpu as pltpu
from jax.sharding import PartitionSpec as P

LX = 32
LY = 16
F32 = jnp.float32
BF16 = jnp.bfloat16
NT = (((1,), (0,)), ((), ()))


def from_behind(array, axis, by):
    count = lax.axis_size(axis)
    return lax.ppermute(array, axis, [(i, (i + by) % count) for i in range(count)])


def plain_link(link, lattice_field):
    result_real = 0.0
    result_imaginary = 0.0
    for column_slot in range(3):
        gauge_link_real = link[None, :, column_slot, 0]
        gauge_link_imaginary = link[None, :, column_slot, 1]
        vector_real = lattice_field[:, None, column_slot, 0]
        vector_imaginary = lattice_field[:, None, column_slot, 1]
        result_real = (
            result_real + gauge_link_real * vector_real - gauge_link_imaginary * vector_imaginary
        )
        result_imaginary = (
            result_imaginary
            + gauge_link_real * vector_imaginary
            + gauge_link_imaginary * vector_real
        )
    return jnp.stack([result_real, result_imaginary], 2)


def adjoint_apply(link, lattice_field):
    result_real = 0.0
    result_imaginary = 0.0
    for column_slot in range(3):
        gauge_link_real = link[None, column_slot, :, 0]
        gauge_link_imaginary = link[None, column_slot, :, 1]
        vector_real = lattice_field[:, None, column_slot, 0]
        vector_imaginary = lattice_field[:, None, column_slot, 1]
        result_real = (
            result_real + gauge_link_real * vector_real + gauge_link_imaginary * vector_imaginary
        )
        result_imaginary = (
            result_imaginary
            + gauge_link_real * vector_imaginary
            - gauge_link_imaginary * vector_real
        )
    return jnp.stack([result_real, result_imaginary], 2)


def cross_parts(left_vec, right_vec):
    reals = []
    imags = []
    for first, second in ((1, 2), (2, 0), (0, 1)):
        ar = left_vec[:, :, first, 0]
        ai = left_vec[:, :, first, 1]
        br = left_vec[:, :, second, 0]
        bi = left_vec[:, :, second, 1]
        cr = right_vec[:, :, first, 0]
        ci = right_vec[:, :, first, 1]
        dr = right_vec[:, :, second, 0]
        di = right_vec[:, :, second, 1]
        reals.append(ar * dr - ai * di - (br * cr - bi * ci))
        imags.append(ar * di + ai * dr - (br * ci + bi * cr))
    return jnp.stack([jnp.stack(reals), jnp.stack(imags)])


def mode_product(lattice_field, block, form):
    high = lax.Precision.HIGHEST
    real_part = jnp.einsum(form, lattice_field[0], block[0], precision=high) - jnp.einsum(
        form, lattice_field[1], block[1], precision=high
    )
    imag_part = jnp.einsum(form, lattice_field[0], block[1], precision=high) + jnp.einsum(
        form, lattice_field[1], block[0], precision=high
    )
    return jnp.stack([real_part, imag_part])


def roll_plane(lattice_field, direction, amount):
    grid = lattice_field.reshape(lattice_field.shape[:-1] + (LY, LX))
    axis_here = grid.ndim - 1 if direction == 0 else grid.ndim - 2
    return jnp.roll(grid, amount, axis_here).reshape(lattice_field.shape)


def elemental_part(phased, vectors):
    count = vectors.shape[0]
    size_a = phased.shape[0]
    nsites = vectors.shape[3]
    real_part = phased[:, :, 0]
    imag_part = phased[:, :, 1]
    upper_rows = jnp.stack([real_part, -imag_part], 1)
    lower_rows = jnp.stack([imag_part, real_part], 1)
    left = jnp.stack([upper_rows, lower_rows], 0).reshape(2 * size_a, 2, 3, nsites)
    width = min(8, count)
    others = vectors.astype(jnp.float32)[None]

    def one_block(rows):
        wmat = cross_parts(rows.astype(jnp.float32)[:, None], others).astype(jnp.bfloat16)
        return jnp.einsum("xrks,rkbcs->xbc", left, wmat, preferred_element_type=jnp.float32)

    result = lax.map(one_block, vectors.reshape(count // width, width, 3, 2, nsites))
    return result.transpose(1, 0, 2, 3).reshape(2, size_a, count * count)


def plain_shards(eigvec, links, momentum, weights, spins, peram):
    local_vecs = eigvec.shape[0]
    planes = eigvec.shape[3]
    plane = eigvec.shape[4]
    depth = planes * lax.axis_size("gz")
    vecf = eigvec.astype(jnp.float32)
    disp = jnp.zeros(vecf.shape, jnp.float32)
    for direction in range(3):
        link = links[direction]
        back = adjoint_apply(link, vecf).astype(jnp.bfloat16)
        if direction == 2:
            upper = from_behind(eigvec, "gz", -1)
            ahead = jnp.concatenate([eigvec[:, :, :, 1:], upper], axis=3).astype(jnp.float32)
            lower = from_behind(back, "gz", 1)
            behind = jnp.concatenate([lower, back[:, :, :, :-1]], axis=3)
        else:
            ahead = roll_plane(vecf, direction, -1)
            behind = roll_plane(back, direction, 1)
        behind = lax.optimization_barrier(behind).astype(jnp.float32)
        factor = weights[direction].astype(jnp.float32)
        disp = disp + factor * (plain_link(link, ahead) - behind)
    sites = jnp.arange(plane, dtype=jnp.int32)
    xcoord = sites % LX
    ycoord = sites // LX
    zcoord = lax.axis_index("gz") * planes + jnp.arange(planes, dtype=jnp.int32)
    two_pi = 2.0 * math.pi
    inplane = (momentum[0] * xcoord).astype(jnp.float32) / LX + (momentum[1] * ycoord).astype(
        jnp.float32
    ) / LY
    angle = (
        two_pi * inplane[None, :]
        + two_pi * (momentum[2] * zcoord).astype(jnp.float32)[:, None] / depth
    )
    cosine = jnp.cos(angle)
    sine = jnp.sin(angle)
    phased_re = cosine * disp[:, :, 0] + sine * disp[:, :, 1]
    phased_im = cosine * disp[:, :, 1] - sine * disp[:, :, 0]
    phased = jnp.stack([phased_re, phased_im], 2).astype(jnp.bfloat16)
    nsites = planes * plane
    phased = phased.reshape(local_vecs, 3, 2, nsites)
    flat_vecs = eigvec.reshape(local_vecs, 3, 2, nsites)
    scale = 1.0 / math.sqrt(LX * LY * depth)
    blocks = [peram[spins[q, 0], spins[q, 1]] for q in range(3)]
    every = lax.all_gather(flat_vecs, "ea", axis=0, tiled=True)
    count = every.shape[0]
    partial_value = elemental_part(phased, every) * scale
    partial_value = partial_value.reshape(2, local_vecs, count, count)
    partial_value = mode_product(partial_value, blocks[2], "abc,cf->abf")
    partial_value = mode_product(partial_value, blocks[1], "abc,be->aec")
    partial_value = partial_value.reshape(2, local_vecs, count * count)
    summed = lax.psum_scatter(partial_value, "gz", scatter_dimension=2, tiled=True)
    rows = lax.dynamic_slice_in_dim(blocks[0], lax.axis_index("ea") * local_vecs, local_vecs, 1)
    term = mode_product(summed, rows, "ak,ad->dk")
    return lax.psum_scatter(term, "ea", scatter_dimension=1, tiled=True)


def split_dot(coeff, field):
    high = coeff.astype(BF16)
    low = (coeff - high.astype(F32)).astype(BF16)
    return lax.dot_general(high, field, NT, preferred_element_type=F32) + lax.dot_general(
        low, field, NT, preferred_element_type=F32
    )


def shift_x(field, ahead, xcoord):
    size = field.shape[-1]
    if ahead:
        return jnp.where(
            xcoord == LX - 1, pltpu.roll(field, LX - 1, 1), pltpu.roll(field, size - 1, 1)
        )
    return jnp.where(xcoord == 0, pltpu.roll(field, size - LX + 1, 1), pltpu.roll(field, 1, 1))


def shift_y(field, ahead):
    size = field.shape[-1]
    return pltpu.roll(field, size - LX if ahead else LX, 1)


def link_times(links, index, field):
    out = []
    for row in range(3):
        re = im = None
        for col in range(3):
            ur, ui = links(*index, row, col)
            vr, vi = field[col]
            a = ur * vr - ui * vi
            b = ur * vi + ui * vr
            re = a if re is None else re + a
            im = b if im is None else im + b
        out.append((re, im))
    return out


def adjoint_times(links, index, field):
    out = []
    for row in range(3):
        re = im = None
        for col in range(3):
            ur, ui = links(*index, col, row)
            vr, vi = field[col]
            a = ur * vr + ui * vi
            b = ur * vi - ui * vr
            re = a if re is None else re + a
            im = b if im is None else im + b
        out.append((re, im))
    return out


def fill_fields(slot, pair, planes, pts, first_row, parity, u_ref, v_ref, rhs_ref, plane):
    rows0 = u_ref.shape[2]
    count = pts.shape[2]

    def turned(which, rows, color):
        fr = planes[slot, :, pl.ds((2 * color) * plane, plane)]
        fi = planes[slot, :, pl.ds((2 * color + 1) * plane, plane)]
        coeff = jnp.concatenate([rows(which, 0), rows(which, 1)], 0)
        n = coeff.shape[0] // 2
        yr = split_dot(coeff, fr)
        yi = split_dot(coeff, fi)
        return yr[:n] - yi[n:], yi[:n] + yr[n:]

    def own_rows(which, part):
        return pts[which, part, pl.ds(first_row, rows0), :]

    def all_rows(which, part):
        return pts[which, part]

    for color in range(3):
        re, im = turned(0, own_rows, color)
        u_ref[slot, 2 * color] = re
        u_ref[slot, 2 * color + 1] = im
        if not pair:
            continue
        at = pl.ds(pl.multiple_of((slot - 1) * plane, plane), plane)
        parts, each = v_ref.shape[1:3]
        re, im = turned(1, all_rows, color)
        for d in range(parts):
            low = slice(2 * d * each, (2 * d + 1) * each)
            high = slice((2 * d + 1) * each, (2 * d + 2) * each)
            vr = jnp.where(parity == 0, re[low], re[high])
            vi = jnp.where(parity == 0, im[low], im[high])
            v_ref[3 * color, d, :, at] = vr
            v_ref[3 * color + 1, d, :, at] = vi
            v_ref[3 * color + 2, d, :, at] = vr + vi
        re, im = turned(2, all_rows, color)
        re = re.astype(BF16)
        im = im.astype(BF16)
        rhs_ref[2 * color, pl.ds(0, count), at] = re
        rhs_ref[2 * color, pl.ds(count, count), at] = im
        rhs_ref[2 * color + 1, pl.ds(0, count), at] = -im
        rhs_ref[2 * color + 1, pl.ds(count, count), at] = re


def displace(weights, phases, links, below, u_ref, p_ref, plane):
    tile = 8
    xcoord = lax.broadcasted_iota(jnp.int32, (tile, plane), 1) % LX

    def one(step, carry):
        rows = pl.ds(pl.multiple_of(step * tile, tile), tile)

        def load(index):
            return [(u_ref[index, 2 * c, rows, :], u_ref[index, 2 * c + 1, rows, :]) for c in range(3)]

        for own in range(2):
            def own_link(direction, row, col, own=own):
                at = ((direction * 3 + row) * 3 + col) * 2
                return links[own, pl.ds(at, 1), :], links[own, pl.ds(at + 1, 1), :]

            def below_link(row, col, own=own):
                if own == 1:
                    return own_link(2, row, col, 0)
                at = (row * 3 + col) * 2
                return below[pl.ds(at, 1), :], below[pl.ds(at + 1, 1), :]

            here = load(own + 1)
            total = [[None, None] for _ in range(3)]
            for direction in range(3):
                if direction == 0:
                    ahead = [(shift_x(r, True, xcoord), shift_x(i, True, xcoord)) for r, i in here]
                    back = adjoint_times(own_link, (0,), here)
                    back = [(shift_x(r, False, xcoord), shift_x(i, False, xcoord)) for r, i in back]
                elif direction == 1:
                    ahead = [(shift_y(r, True), shift_y(i, True)) for r, i in here]
                    back = adjoint_times(own_link, (1,), here)
                    back = [(shift_y(r, False), shift_y(i, False)) for r, i in back]
                else:
                    ahead = load(own + 2)
                    back = adjoint_times(below_link, (), load(own))
                front = link_times(own_link, (direction,), ahead)
                factor = weights[direction].astype(F32)
                for k in range(3):
                    for c in range(2):
                        term = factor * (front[k][c] - back[k][c])
                        total[k][c] = term if total[k][c] is None else total[k][c] + term
            cosine, sine = phases[own]
            at = pl.ds(own * plane, plane)
            for k in range(3):
                re = cosine * total[k][0] + sine * total[k][1]
                im = cosine * total[k][1] - sine * total[k][0]
                p_ref[3 * k, rows, at] = re
                p_ref[3 * k + 1, rows, at] = im
                p_ref[3 * k + 2, rows, at] = re + im
        return carry

    lax.fori_loop(0, p_ref.shape[1] // tile, one, 0)


def cross_tile(m_ref, p_ref, v_ref, part, lanes, lane, r):
    rows = p_ref.shape[1]
    at = pl.ds(pl.multiple_of(lanes + lane, 128), 128)
    p = [p_ref[c, pl.ds(r, 16), at] for c in range(9)]
    for b in range(v_ref.shape[2]):
        v = [v_ref[c, part, pl.ds(b, 1), at] for c in range(9)]
        to = pl.ds(pl.multiple_of(b * rows + r, 16), 16)
        for j in range(3):
            k, i = (j + 1) % 3, (j + 2) % 3
            t = [p[3 * k + s] * v[3 * i + s] - p[3 * i + s] * v[3 * k + s] for s in range(3)]
            re = t[0] - t[1]
            im = t[2] - (t[0] + t[1])
            m_ref[2 * j, to, pl.ds(lane, 128)] = re.astype(BF16)
            m_ref[2 * j + 1, to, pl.ds(lane, 128)] = im.astype(BF16)


def mixed(next_ref, now_ref, p_ref, v_ref, rhs_ref, acc, part, lanes, now_lanes, now_first):
    width = next_ref.shape[2]
    rows = p_ref.shape[1]
    at = pl.ds(pl.multiple_of(now_lanes, 128), width)

    def body(t, carry):
        r = pl.multiple_of(t * 16, 16)
        for lane in range(0, width, 128):
            cross_tile(next_ref, p_ref, v_ref, part, lanes, lane, r)
        total = None
        for j in range(2):
            term = lax.dot_general(
                now_ref[2 * t + j],
                rhs_ref[2 * t + j, :, at],
                (((1,), (1,)), ((), ())),
                preferred_element_type=F32,
            )
            total = term if total is None else total + term
        keep = jnp.where(jnp.logical_and(now_first, t == 0), 0.0, 1.0)
        acc[...] = acc[...] * keep + total
        return carry

    lax.fori_loop(0, 3, body, 0)


def block_kernel(names, weights, momentum, own_ref, links_ref, zlinks_ref, pts, o_ref, planes, links,
                 below, u_ref, p_ref, v_ref, rhs_ref, acc, m0, m1, stage, arrived, psend, precv, ssend,
                 srecv, lsend, lrecv, bsend, brecv, rsend, rrecv):
    gz, ea, ndev = names
    me = lax.axis_index(gz)
    core = lax.axis_index(ea)
    odd = me % 2
    half = ndev // 2
    local, width6 = own_ref.shape
    plane = width6 // 6

    def at_gz(index):
        return {gz: index}

    sibling = {ea: 1 - core}
    mate = me + 1 - 2 * odd
    side = lax.rem(me + ndev - 1 + 2 * odd, ndev)
    jump = lax.rem(me + ndev - 2 + 4 * odd, ndev)

    def same_parity(t):
        return lax.rem(me + 2 * t, ndev)

    barrier = pltpu.get_barrier_semaphore()
    friends = [sibling, at_gz(mate), at_gz(side)] + [at_gz(same_parity(t)) for t in range(1, half)]
    for friend in friends:
        pl.semaphore_signal(barrier, inc=1, device_id=friend, device_id_type=pl.DeviceIdType.MESH)
    pl.semaphore_wait(barrier, len(friends))

    mine = pl.ds(pl.multiple_of(core * local, 16), local)
    my_slot = 1 + odd
    mate_slot = 2 - odd
    out_slot = 3 - 3 * odd

    def remote(src, dst, send, recv, device):
        return pltpu.make_async_remote_copy(
            src_ref=src, dst_ref=dst, send_sem=send, recv_sem=recv, device_id=device,
            device_id_type=pl.DeviceIdType.MESH,
        )

    share = remote(own_ref, planes.at[my_slot, mine], ssend.at[my_slot], srecv.at[my_slot], sibling)
    share.start()
    to_mate = remote(own_ref, planes.at[my_slot, mine], psend.at[0], precv.at[my_slot], at_gz(mate))
    to_mate.start()
    to_side = remote(own_ref, planes.at[out_slot, mine], psend.at[1], precv.at[out_slot], at_gz(side))
    to_jump = remote(own_ref, planes.at[out_slot, mine], psend.at[2], precv.at[out_slot], at_gz(jump))
    to_side.start()
    to_jump.start()
    link_mate = remote(links_ref, links.at[odd], lsend, lrecv.at[odd], at_gz(mate))
    link_mate.start()
    z_side = remote(zlinks_ref, below, bsend.at[0], brecv, at_gz(side))
    z_jump = remote(zlinks_ref, below, bsend.at[1], brecv, at_gz(jump))

    @pl.when(odd == 1)
    def _():
        z_side.start()
        z_jump.start()

    planes[my_slot, mine, :] = own_ref[...]
    links[odd] = links_ref[...]

    def landed(slot, recv):
        return remote(own_ref, planes.at[slot, mine], psend.at[0], recv.at[slot], sibling)

    def fill(slot, pair):
        fill_fields(slot, pair, planes, pts, pl.multiple_of(core * local, 8), odd, u_ref, v_ref,
                    rhs_ref, plane)

    def theirs(slot):
        rows = pl.ds(pl.multiple_of((1 - core) * local, 16), local)
        return remote(own_ref, planes.at[slot, rows], psend.at[0], srecv.at[slot], sibling)

    theirs(my_slot).wait_recv()
    fill(my_slot, True)
    for slot, pair in ((mate_slot, True), (0, False), (3, False)):
        landed(slot, precv).wait_recv()
        block = planes.at[slot, mine]
        remote(block, block, ssend.at[slot], srecv.at[slot], sibling).start()
        theirs(slot).wait_recv()
        fill(slot, pair)
    remote(links_ref, links.at[1 - odd], lsend, lrecv.at[1 - odd], at_gz(mate)).wait_recv()
    z_side.wait_recv()

    sites = lax.broadcasted_iota(jnp.int32, (1, plane), 1)
    two_pi = 2.0 * math.pi
    scale = 1.0 / math.sqrt(plane * ndev)
    inplane = (momentum[0] * (sites % LX)).astype(F32) / LX + (
        momentum[1] * (sites // LX)
    ).astype(F32) / LY
    phases = []
    for own in range(2):
        height = jnp.full((1, plane), momentum[2] * (me - odd + own), jnp.int32).astype(F32)
        angle = two_pi * inplane + two_pi * height / ndev
        phases.append((jnp.cos(angle) * scale, jnp.sin(angle) * scale))
    displace(weights, phases, links, below, u_ref, p_ref, plane)

    width = m0.shape[2]
    chunks = p_ref.shape[2] // width
    total = half * chunks
    zplace = me // 2

    def place(n):
        return lax.rem(zplace + 1 + n // chunks, half), (n % chunks) * width

    part, lanes = place(0)

    def begin(t, carry):
        for lane in range(0, width, 128):
            cross_tile(m0, p_ref, v_ref, part, lanes, lane, pl.multiple_of(t * 16, 16))
        return carry

    lax.fori_loop(0, 3, begin, 0)
    short = acc.shape[0] // 2
    wide = acc.shape[1]

    def send(t):
        return remote(stage.at[t], arrived.at[t], rsend.at[t], rrecv.at[t], at_gz(same_parity(t + 1)))

    def stretch(n, carry):
        for sub, (now, after) in enumerate(((m0, m1), (m1, m0))):
            step = 2 * n + sub
            now_part, now_lanes = place(step)
            part, lanes = place(jnp.minimum(step + 1, total - 1))
            mixed(after, now, p_ref, v_ref, rhs_ref, acc, part, lanes, now_lanes, step % chunks == 0)
        return carry

    def one_part(d, carry):
        lax.fori_loop(d * (chunks // 2), (d + 1) * (chunks // 2), stretch, 0)

        @pl.when(d < half - 1)
        def _():
            stage[d, :, pl.ds(0, wide)] = acc[pl.ds(0, short), :].astype(BF16)
            stage[d, :, pl.ds(wide, wide)] = acc[pl.ds(short, short), :].astype(BF16)
            send(d).start()

        return carry

    lax.fori_loop(0, half, one_part, 0)
    o_ref[:, pl.ds(0, wide)] = acc[pl.ds(0, short), :]
    o_ref[:, pl.ds(wide, wide)] = acc[pl.ds(short, short), :]
    for t in range(half - 1):
        send(t).wait_recv()
        o_ref[...] += arrived[t].astype(F32)
    for t in range(half - 1):
        send(t).wait_send()
    to_mate.wait_send()
    to_side.wait_send()
    to_jump.wait_send()
    link_mate.wait_send()
    for slot in range(4):
        block = planes.at[slot, mine]
        remote(block, block, ssend.at[slot], srecv.at[slot], sibling).wait_send()

    @pl.when(odd == 1)
    def _():
        z_side.wait_send()
        z_jump.wait_send()


def shards(eigvec, links, momentum, weights, spins, peram):
    local = eigvec.shape[0]
    plane = eigvec.shape[4]
    ndev = lax.axis_size("gz")
    count = peram.shape[-1]
    each = count // ndev
    half = ndev // 2
    own = eigvec.reshape(local, 6 * plane)
    mylinks = links.reshape(54, plane)
    pts = jnp.stack([peram[spins[q, 0], spins[q, 1]] for q in range(3)]).swapaxes(2, 3)
    vmem = pl.BlockSpec(memory_space=pltpu.VMEM)
    smem = pl.BlockSpec(memory_space=pltpu.SMEM)
    total = 2 * plane
    width = 256
    rows = each * local
    dma = pltpu.SemaphoreType.DMA
    out = pl.pallas_call(
        functools.partial(block_kernel, ("gz", "ea", ndev)),
        out_shape=jax.ShapeDtypeStruct((rows // 2, 4 * count), F32),
        in_specs=[smem, smem, vmem, vmem, vmem, vmem],
        out_specs=vmem,
        scratch_shapes=[
            pltpu.VMEM((4, 2 * local, 6 * plane), BF16),
            pltpu.VMEM((2, 54, plane), F32),
            pltpu.VMEM((18, plane), F32),
            pltpu.VMEM((4, 6, local, plane), F32),
            pltpu.VMEM((9, local, total), F32),
            pltpu.VMEM((9, half, each, total), F32),
            pltpu.VMEM((6, 2 * count, total), BF16),
            pltpu.VMEM((rows, 2 * count), F32),
            pltpu.VMEM((6, rows, width), BF16),
            pltpu.VMEM((6, rows, width), BF16),
            pltpu.VMEM((half - 1, rows // 2, 4 * count), BF16),
            pltpu.VMEM((half - 1, rows // 2, 4 * count), BF16),
            dma((3,)),
            dma((4,)),
            dma((4,)),
            dma((4,)),
            dma,
            dma((2,)),
            dma((2,)),
            dma,
            dma((half - 1,)),
            dma((half - 1,)),
        ],
        compiler_params=pltpu.CompilerParams(
            vmem_limit_bytes=62 * 1024 * 1024, collective_id=0, has_side_effects=True
        ),
        name="block",
    )(weights, momentum, own, mylinks, mylinks[36:], pts)
    out = out.reshape(each // 2, local, 2, 2, count).transpose(3, 1, 2, 0, 4)
    return out.reshape(2, local, each * count)


def solution(mesh):
    ndev = mesh.shape["gz"]
    in_specs = (
        P("ea", None, None, ("groups", "gz"), None),
        P(None, None, None, None, ("groups", "gz"), None),
        P("groups"),
        P("groups"),
        P("groups", None),
        P("groups", None, None, None, None),
    )
    out_specs = P("groups", "ea", "gz")

    def body(eigvec, links, momentum, weights, spins, peram):
        whole_rows = peram.shape[-1] % (2 * ndev) == 0 and ndev % 2 == 0 and ndev > 2
        whole_rows = whole_rows and eigvec.shape[3] == 1
        run = shards if whole_rows else plain_shards
        return run(eigvec, links, momentum, weights, spins, peram)

    return jax.shard_map(body, mesh=mesh, in_specs=in_specs, out_specs=out_specs, check_vma=False)
```

profile of v0, /device:TPU:0, one launch (start us, length us, event | category | flops | bytes accessed | tf_op | source)
XLA Modules:
  0.0 87.5 jit_solution(10601235515431480343)
XLA Ops:
  0.0 0.0 copy-start
  0.0 1.6 %fusion = (s32[1,1]{0,1:T(1,128)}, s32[1,1]{0,1:T(1,128)}, s32[1,1]{0,1:T(1,128)}, s32[1,1]{0,1:T(1,128)}, s32[1,1]{0,1:T(1,128)}, /*index=5*/s32[1,1]{0,1:T(1,128)}) fusion(s32[3,2]{0,1:T(2,128)} %param.10), kind=kLoop, calls=%fused_computation.6 | loop fusion | bytes 48 | tf_op jit(solution)/shard_map/slice | solution.py:530
  12.9 0.9 %slice_reduce_fusion = f32[3,3,2,512]{3,2,1,0:T(2,128)S(1)} fusion(f32[3,3,3,2,1,512]{5,4,3,2,1,0:T(1,128)} %param.7), kind=kLoop, calls=%fused_computation.2 | loop fusion | bytes 73728 | tf_op jit(solution)/shard_map/slice | solution.py:570
  13.8 0.6 slice.25.zlinks_ref
  14.4 1.2 %reduce = f32[3,3,3,2,512]{4,3,2,1,0:T(2,128)S(1)} reduce(f32[3,3,3,2,1,512]{5,4,3,2,1,0:T(1,128)} %param.7, f32[]{:T(128)} %constant.9), dimensions={4}, to_apply=%param.7.reduce_sub_computation | reduce | bytes 221188 | tf_op args[1]
  15.6 0.7 reshape.14.links_ref
  16.3 1.0 %constant_dynamic-slice_fusion.2 = (f32[1,1,2,96,96]{4,3,2,1,0:T(8,128)S(1)}, f32[1,1,2,96,96]{4,3,2,1,0:T(8,128)S(1)}, f32[1,1,2,96,96]{4,3,2,1,0:T(8,128)S(1)}) fusion(f32[4,4,2,96,96]{4,3,2,1,0:T(8,128)} %param.11, s32[]{:T(128)S(6)} %select_n.18, s32[]{:T(128)S(6)} %select_n.19, s32[]{:T(128)S(6)} %select_n.22, s32[]{:T(128)S(6)} %select_n.23, ...), kind=kLoop, calls=%fused_computation.5 | loop fusion | bytes 442392 | tf_op jit(solution)/shard_map/dynamic_slice | solution.py:530
  17.4 0.1 copy.11
  17.5 0.1 copy.13
  17.5 0.1 copy.12
  17.6 0.7 maximum_bitcast_fusion.pts
  18.4 0.0 copy-done
  18.4 0.9 %reshape.13.own_ref = bf16[48,3072]{1,0:T(8,128)(2,1)} reshape(bf16[48,3,2,1,512]{4,2,3,1,0:T(2,128)(2,1)S(1)} %copy-done) | data formatting | bytes 589824 | tf_op jit(solution)/shard_map/reshape | solution.py:528
  19.3 65.1 %block.1 = f32[288,384]{1,0:T(8,128)} custom-call(s32[3]{0:T(128)} %weights.1, s32[3]{0:T(128)} %momentum.1, bf16[48,3072]{1,0:T(8,128)(2,1)} %reshape.13.own_ref, f32[54,512]{1,0:T(8,128)} %reshape.14.links_ref, f32[18,512]{1,0:T(8,128)} %slice.25.zlinks_ref, f32[3,2,96,96]{3,2,1,0:T(8,128)} %maximum_bitcast_fusion.pts), custom_call_target="tpu_custom_call" | custom-call | tf_op jit(solution)/shard_map/block/pallas_call | solution.py:537
  84.4 1.7 %reshape.15 = f32[6,48,2,2,96]{4,3,2,1,0:T(2,128)S(1)} reshape(f32[288,384]{1,0:T(8,128)} %block.1) | data formatting | bytes 884736 | tf_op jit(solution)/shard_map/reshape | solution.py:571
  86.1 0.4 copy.18
  86.4 1.1 %reshape.16 = f32[2,48,1152]{2,1,0:T(8,128)} reshape(f32[2,48,2,6,96]{4,3,2,1,0:T(8,128)S(1)} %bitcast.16) | data formatting | bytes 884736 | tf_op jit(solution)/shard_map/reshape | solution.py:572
Async XLA Ops:
  0.0 18.4 %copy-start = (bf16[48,3,2,1,512]{4,2,3,1,0:T(2,128)(2,1)S(1)}, bf16[48,3,2,1,512]{4,2,3,1,0:T(2,128)(2,1)}, u32[]{:S(2)}) copy-start(bf16[48,3,2,1,512]{4,2,3,1,0:T(2,128)(2,1)} %param.6) | copy-start | bytes 884740
where the time goes:
time: 88 us; the launch traced here: 87.5 us
  Pallas kernels  65.1 us (74%)
  between operations  11.4 us (13%)
  local copies, waits for them, and re-layouts  9.08 us (10%)
  other arithmetic  1.95 us (2%)
    pallas_call x1, Pallas kernels, shards(): pl.pallas_call(functools.partial(block_kernel, ('gz', 'ea', ndev)), out_s...  65.1 us
    reshape x2, local copies, waits for them, and re-layouts, shards(): out = out.reshape(each // 2, local, 2, 2, count).transpose(3, 1, 2, 0, 4)  2.02 us

commit v1 on v0

--- a/solution.py
+++ b/solution.py
@@ -277,14 +277,12 @@
 
         for own in range(2):
             def own_link(direction, row, col, own=own):
-                at = ((direction * 3 + row) * 3 + col) * 2
-                return links[own, pl.ds(at, 1), :], links[own, pl.ds(at + 1, 1), :]
+                return tuple(links[own, direction, row, col, c] for c in range(2))
 
             def below_link(row, col, own=own):
                 if own == 1:
                     return own_link(2, row, col, 0)
-                at = (row * 3 + col) * 2
-                return below[pl.ds(at, 1), :], below[pl.ds(at + 1, 1), :]
+                return tuple(below[row, col, c] for c in range(2))
 
             here = load(own + 1)
             total = [[None, None] for _ in range(3)]
@@ -341,9 +339,6 @@
     at = pl.ds(pl.multiple_of(now_lanes, 128), width)
 
     def body(t, carry):
-        r = pl.multiple_of(t * 16, 16)
-        for lane in range(0, width, 128):
-            cross_tile(next_ref, p_ref, v_ref, part, lanes, lane, r)
         total = None
         for j in range(2):
             term = lax.dot_general(
@@ -353,6 +348,9 @@
                 preferred_element_type=F32,
             )
             total = term if total is None else total + term
+        r = pl.multiple_of(t * 16, 16)
+        for lane in range(0, width, 128):
+            cross_tile(next_ref, p_ref, v_ref, part, lanes, lane, r)
         keep = jnp.where(jnp.logical_and(now_first, t == 0), 0.0, 1.0)
         acc[...] = acc[...] * keep + total
         return carry
@@ -360,9 +358,9 @@
     lax.fori_loop(0, 3, body, 0)
 
 
-def block_kernel(names, weights, momentum, own_ref, links_ref, zlinks_ref, pts, o_ref, planes, links,
-                 below, u_ref, p_ref, v_ref, rhs_ref, acc, m0, m1, stage, arrived, psend, precv, ssend,
-                 srecv, lsend, lrecv, bsend, brecv, rsend, rrecv):
+def block_kernel(names, weights, momentum, spins, own_ref, links_ref, peram_hbm, o_ref, peram, pts,
+                 planes, links, below, u_ref, p_ref, v_ref, rhs_ref, acc, m0, m1, stage, arrived, psend, precv, ssend,
+                 srecv, lsend, lrecv, bsend, brecv, rsend, rrecv, jsend, jrecv, xsend, xrecv, csem):
     gz, ea, ndev = names
     me = lax.axis_index(gz)
     core = lax.axis_index(ea)
@@ -376,22 +374,32 @@
 
     sibling = {ea: 1 - core}
     mate = me + 1 - 2 * odd
-    side = lax.rem(me + ndev - 1 + 2 * odd, ndev)
     jump = lax.rem(me + ndev - 2 + 4 * odd, ndev)
+    fetch = pltpu.make_async_copy(peram_hbm, peram, csem)
+    fetch.start()
 
     def same_parity(t):
         return lax.rem(me + 2 * t, ndev)
 
     barrier = pltpu.get_barrier_semaphore()
-    friends = [sibling, at_gz(mate), at_gz(side)] + [at_gz(same_parity(t)) for t in range(1, half)]
+    friends = [sibling, at_gz(mate)] + [at_gz(same_parity(t)) for t in range(1, half)]
     for friend in friends:
         pl.semaphore_signal(barrier, inc=1, device_id=friend, device_id_type=pl.DeviceIdType.MESH)
     pl.semaphore_wait(barrier, len(friends))
 
-    mine = pl.ds(pl.multiple_of(core * local, 16), local)
+    piece = 16
+    pieces = local // piece
+    my_first = core * local
+    her_first = (1 - core) * local
     my_slot = 1 + odd
     mate_slot = 2 - odd
-    out_slot = 3 - 3 * odd
+    jump_slot = 3 - 3 * odd
+    far_slot = 3 * odd
+
+    def span(first, n=None):
+        if n is None:
+            return pl.ds(pl.multiple_of(first, 16), local)
+        return pl.ds(pl.multiple_of(first + n * piece, 16), piece)
 
     def remote(src, dst, send, recv, device):
         return pltpu.make_async_remote_copy(
@@ -399,48 +407,86 @@
             device_id_type=pl.DeviceIdType.MESH,
         )
 
-    share = remote(own_ref, planes.at[my_slot, mine], ssend.at[my_slot], srecv.at[my_slot], sibling)
-    share.start()
-    to_mate = remote(own_ref, planes.at[my_slot, mine], psend.at[0], precv.at[my_slot], at_gz(mate))
+    def to_jump(n):
+        return remote(
+            own_ref.at[pl.ds(n * piece, piece)], planes.at[jump_slot, span(my_first, n)],
+            jsend.at[n], jrecv.at[n], at_gz(jump),
+        )
+
+    def z_links():
+        return remote(links_ref.at[2], below, bsend, brecv, at_gz(jump))
+
+    def z_relay():
+        return remote(below, below, bsend, brecv, at_gz(mate))
+
+    def relay(slot, n):
+        block = planes.at[slot, span(my_first, n)]
+        return remote(block, block, xsend.at[n], xrecv.at[n], at_gz(mate))
+
+    def share(slot, first):
+        block = planes.at[slot, span(first)]
+        return remote(block, block, ssend.at[slot], srecv.at[slot], sibling)
+
+    for n in range(pieces):
+        to_jump(n).start()
+
+    @pl.when(odd == 1)
+    def _():
+        z_links().start()
+
+    share_own = remote(
+        own_ref, planes.at[my_slot, span(my_first)], ssend.at[my_slot], srecv.at[my_slot], sibling
+    )
+    share_own.start()
+    to_mate = remote(own_ref, planes.at[my_slot, span(my_first)], psend, precv, at_gz(mate))
     to_mate.start()
-    to_side = remote(own_ref, planes.at[out_slot, mine], psend.at[1], precv.at[out_slot], at_gz(side))
-    to_jump = remote(own_ref, planes.at[out_slot, mine], psend.at[2], precv.at[out_slot], at_gz(jump))
-    to_side.start()
-    to_jump.start()
     link_mate = remote(links_ref, links.at[odd], lsend, lrecv.at[odd], at_gz(mate))
     link_mate.start()
-    z_side = remote(zlinks_ref, below, bsend.at[0], brecv, at_gz(side))
-    z_jump = remote(zlinks_ref, below, bsend.at[1], brecv, at_gz(jump))
+    planes[my_slot, span(my_first), :] = own_ref[...]
+    links[odd] = links_ref[...]
+    fetch.wait()
+    for q in range(3):
+        for c in range(2):
+            pts[q, c] = peram[spins[q, 0], spins[q, 1], c].T
+
+    def fill(slot, pair):
+        fill_fields(slot, pair, planes, pts, pl.multiple_of(my_first, 8), odd, u_ref, v_ref,
+                    rhs_ref, plane)
+
+    share(my_slot, her_first).wait_recv()
+    fill(my_slot, True)
+    to_jump(0).wait_recv()
+    relay(jump_slot, 0).start()
+    remote(own_ref, planes.at[mate_slot, span(my_first)], psend, precv, at_gz(mate)).wait_recv()
+    share(mate_slot, my_first).start()
+    for n in range(1, pieces - 1):
+        to_jump(n).wait_recv()
+        relay(jump_slot, n).start()
+    share(mate_slot, her_first).wait_recv()
+    fill(mate_slot, True)
+    for n in range(max(pieces - 1, 1), pieces):
+        to_jump(n).wait_recv()
+        relay(jump_slot, n).start()
+    share(jump_slot, my_first).start()
 
     @pl.when(odd == 1)
     def _():
-        z_side.start()
-        z_jump.start()
-
-    planes[my_slot, mine, :] = own_ref[...]
-    links[odd] = links_ref[...]
-
-    def landed(slot, recv):
-        return remote(own_ref, planes.at[slot, mine], psend.at[0], recv.at[slot], sibling)
-
-    def fill(slot, pair):
-        fill_fields(slot, pair, planes, pts, pl.multiple_of(core * local, 8), odd, u_ref, v_ref,
-                    rhs_ref, plane)
-
-    def theirs(slot):
-        rows = pl.ds(pl.multiple_of((1 - core) * local, 16), local)
-        return remote(own_ref, planes.at[slot, rows], psend.at[0], srecv.at[slot], sibling)
-
-    theirs(my_slot).wait_recv()
-    fill(my_slot, True)
-    for slot, pair in ((mate_slot, True), (0, False), (3, False)):
-        landed(slot, precv).wait_recv()
-        block = planes.at[slot, mine]
-        remote(block, block, ssend.at[slot], srecv.at[slot], sibling).start()
-        theirs(slot).wait_recv()
-        fill(slot, pair)
+        z_links().wait_send()
+        z_links().wait_recv()
+        z_relay().start()
+
+    @pl.when(odd == 0)
+    def _():
+        z_relay().wait_recv()
+
+    share(jump_slot, her_first).wait_recv()
+    fill(jump_slot, False)
+    for n in range(pieces):
+        relay(far_slot, n).wait_recv()
+    share(far_slot, my_first).start()
+    share(far_slot, her_first).wait_recv()
+    fill(far_slot, False)
     remote(links_ref, links.at[1 - odd], lsend, lrecv.at[1 - odd], at_gz(mate)).wait_recv()
-    z_side.wait_recv()
 
     sites = lax.broadcasted_iota(jnp.int32, (1, plane), 1)
     two_pi = 2.0 * math.pi
@@ -471,8 +517,13 @@
         return carry
 
     lax.fori_loop(0, 3, begin, 0)
-    short = acc.shape[0] // 2
-    wide = acc.shape[1]
+    rows = p_ref.shape[1]
+    wide = acc.shape[1] // 2
+
+    def lay_out(put):
+        for b in range(v_ref.shape[2]):
+            for c in range(2):
+                put(c, pl.ds(b * wide, wide), acc[pl.ds(b * rows, rows), pl.ds(c * wide, wide)])
 
     def send(t):
         return remote(stage.at[t], arrived.at[t], rsend.at[t], rrecv.at[t], at_gz(same_parity(t + 1)))
@@ -490,32 +541,36 @@
 
         @pl.when(d < half - 1)
         def _():
-            stage[d, :, pl.ds(0, wide)] = acc[pl.ds(0, short), :].astype(BF16)
-            stage[d, :, pl.ds(wide, wide)] = acc[pl.ds(short, short), :].astype(BF16)
+            def put(c, at, block):
+                stage[d, c, :, at] = block.astype(BF16)
+
+            lay_out(put)
             send(d).start()
 
         return carry
 
     lax.fori_loop(0, half, one_part, 0)
-    o_ref[:, pl.ds(0, wide)] = acc[pl.ds(0, short), :]
-    o_ref[:, pl.ds(wide, wide)] = acc[pl.ds(short, short), :]
+
+    def put_own(c, at, block):
+        o_ref[c, :, at] = block
+
+    lay_out(put_own)
     for t in range(half - 1):
         send(t).wait_recv()
         o_ref[...] += arrived[t].astype(F32)
     for t in range(half - 1):
         send(t).wait_send()
     to_mate.wait_send()
-    to_side.wait_send()
-    to_jump.wait_send()
     link_mate.wait_send()
+    for n in range(pieces):
+        to_jump(n).wait_send()
+        relay(jump_slot, n).wait_send()
     for slot in range(4):
-        block = planes.at[slot, mine]
-        remote(block, block, ssend.at[slot], srecv.at[slot], sibling).wait_send()
+        share(slot, my_first).wait_send()
 
     @pl.when(odd == 1)
     def _():
-        z_side.wait_send()
-        z_jump.wait_send()
+        z_relay().wait_send()
 
 
 def shards(eigvec, links, momentum, weights, spins, peram):
@@ -526,8 +581,6 @@
     each = count // ndev
     half = ndev // 2
     own = eigvec.reshape(local, 6 * plane)
-    mylinks = links.reshape(54, plane)
-    pts = jnp.stack([peram[spins[q, 0], spins[q, 1]] for q in range(3)]).swapaxes(2, 3)
     vmem = pl.BlockSpec(memory_space=pltpu.VMEM)
     smem = pl.BlockSpec(memory_space=pltpu.SMEM)
     total = 2 * plane
@@ -536,13 +589,15 @@
     dma = pltpu.SemaphoreType.DMA
     out = pl.pallas_call(
         functools.partial(block_kernel, ("gz", "ea", ndev)),
-        out_shape=jax.ShapeDtypeStruct((rows // 2, 4 * count), F32),
-        in_specs=[smem, smem, vmem, vmem, vmem, vmem],
+        out_shape=jax.ShapeDtypeStruct((2, local, each * count), F32),
+        in_specs=[smem, smem, smem, vmem, vmem, pl.BlockSpec(memory_space=pl.ANY)],
         out_specs=vmem,
         scratch_shapes=[
+            pltpu.VMEM(peram.shape, F32),
+            pltpu.VMEM((3, 2, count, count), F32),
             pltpu.VMEM((4, 2 * local, 6 * plane), BF16),
-            pltpu.VMEM((2, 54, plane), F32),
-            pltpu.VMEM((18, plane), F32),
+            pltpu.VMEM((2,) + links.shape, F32),
+            pltpu.VMEM(links.shape[1:], F32),
             pltpu.VMEM((4, 6, local, plane), F32),
             pltpu.VMEM((9, local, total), F32),
             pltpu.VMEM((9, half, each, total), F32),
@@ -550,26 +605,30 @@
             pltpu.VMEM((rows, 2 * count), F32),
             pltpu.VMEM((6, rows, width), BF16),
             pltpu.VMEM((6, rows, width), BF16),
-            pltpu.VMEM((half - 1, rows // 2, 4 * count), BF16),
-            pltpu.VMEM((half - 1, rows // 2, 4 * count), BF16),
-            dma((3,)),
-            dma((4,)),
+            pltpu.VMEM((half - 1, 2, local, each * count), BF16),
+            pltpu.VMEM((half - 1, 2, local, each * count), BF16),
+            dma,
+            dma,
             dma((4,)),
             dma((4,)),
             dma,
             dma((2,)),
-            dma((2,)),
+            dma,
             dma,
             dma((half - 1,)),
             dma((half - 1,)),
+            dma((local // 16,)),
+            dma((local // 16,)),
+            dma((local // 16,)),
+            dma((local // 16,)),
+            dma,
         ],
         compiler_params=pltpu.CompilerParams(
             vmem_limit_bytes=62 * 1024 * 1024, collective_id=0, has_side_effects=True
         ),
         name="block",
-    )(weights, momentum, own, mylinks, mylinks[36:], pts)
-    out = out.reshape(each // 2, local, 2, 2, count).transpose(3, 1, 2, 0, 4)
-    return out.reshape(2, local, each * count)
+    )(weights, momentum, spins, own, links, peram)
+    return out
 
 
 def solution(mesh):
@@ -586,7 +645,7 @@
 
     def body(eigvec, links, momentum, weights, spins, peram):
         whole_rows = peram.shape[-1] % (2 * ndev) == 0 and ndev % 2 == 0 and ndev > 2
-        whole_rows = whole_rows and eigvec.shape[3] == 1
+        whole_rows = whole_rows and eigvec.shape[0] % 16 == 0 and eigvec.shape[3] == 1
         run = shards if whole_rows else plain_shards
         return run(eigvec, links, momentum, weights, spins, peram)
 

time: 88 us -> 67.2 us (0.76)
  between operations: 11.4 us -> 0.01 us
  local copies, waits for them, and re-layouts: 9.08 us -> 5.02 us
  Pallas kernels: 65.1 us -> 62 us
  other arithmetic: 1.95 us -> 0 us
    reshape x4 -> x0, local copies, waits for them, and re-layouts: 3.8 us -> none  [the longest x2 2.02 us: shards(): out = out.reshape(each // 2, local, 2, 2, count).transpose(3, 1, 2, 0, 4)]
    unnamed x2, local copies, waits for them, and re-layouts: 0.01 us -> 3.14 us
    pallas_call x1, Pallas kernels: 65.1 us -> 62 us  [shards(): pl.pallas_call(functools.partial(block_kernel, ('gz', 'ea', ndev)), out_s...]
    slice x3 -> x0, local copies, waits for them, and re-layouts: 3.09 us -> none  [the longest x1 1.56 us: shards(): spins[q, 1]]
    dynamic_slice x4 -> x0, local copies, waits for them, and re-layouts: 1.27 us -> none  [shards(): peram[spins[q, 0], spins[q, 1]]]
    unnamed x1 -> x0, other arithmetic: 1.22 us -> none
    reshape x1, local copies, waits for them, and re-layouts: 0.92 us -> 1.87 us  [shards(): own = eigvec.reshape(local, 6 * plane)]
where the time goes in v1:
time: 67.2 us; the launch traced here: 67 us
  Pallas kernels  62 us (92%)
  local copies, waits for them, and re-layouts  5.02 us (7%)
    pallas_call x1, Pallas kernels, shards(): pl.pallas_call(functools.partial(block_kernel, ('gz', 'ea', ndev)), out_s...  62 us
    unnamed x2, local copies, waits for them, and re-layouts  3.14 us
    reshape x1, local copies, waits for them, and re-layouts, shards(): own = eigvec.reshape(local, 6 * plane)  1.87 us

profile of v1, /device:TPU:0, one launch (start us, length us, event | category | flops | bytes accessed | tf_op | source)
XLA Modules:
  0.0 67.0 jit_solution(12893712113100984954)
XLA Ops:
  0.0 1.3 %copy.7.spins = s32[3,2]{1,0:T(4,128)} copy(s32[3,2]{0,1:T(2,128)} %param.10) | data formatting | bytes 48 | tf_op args[4]
  1.3 1.9 %reshape.3.own_ref = bf16[48,3072]{1,0:T(8,128)(2,1)} reshape(bf16[48,3,2,1,512]{4,2,3,1,0:T(2,128)(2,1)} %param.6) | data formatting | bytes 589824 | tf_op jit(solution)/shard_map/reshape | solution.py:583
  3.2 62.0 %block.1 = f32[2,48,1152]{2,1,0:T(8,128)} custom-call(s32[3]{0:T(128)} %weights.1, s32[3]{0:T(128)} %momentum.1, s32[3,2]{1,0:T(4,128)} %copy.7.spins, bf16[48,3072]{1,0:T(8,128)(2,1)} %reshape.3.own_ref, f32[3,3,3,2,1,512]{5,4,3,2,1,0:T(1,128)} %links_ref.1, f32[4,4,2,96,96]{4,3,2,1,0:T(8,128)} %peram_hbm.1), custom_call_target="tpu_custom_call" | custom-call | tf_op jit(solution)/shard_map/block/pallas_call | solution.py:590
  65.2 1.8 %copy.9 = f32[2,48,1152]{2,1,0:T(8,128)} copy(f32[2,48,1152]{2,1,0:T(8,128)} %block.1) | data formatting | bytes 884736
